TPU v7x, 32 devices: a whole 2x2x4 slice. The times are simulated.
32 devices in a mesh: mem: 8 (over y, x, core), tile: 4 (over z).
Axes of the slice: x: 2, y: 2, z: 4, core: 2. Of those that a mesh axis runs over, the one named last changes fastest.
Arguments:
- perturbations: bfloat16 [16, 4, 128, 1024], P('mem', None, 'tile'), may hold values from -6 to 6
- right_side: float32 [4, 128, 1024], P(None, 'tile'), may hold values from -14 to 14
- fine_taps: float32 [2, 4, 5], replicated, may hold values from 0.3 to 1
- coarse_lat: float32 [32, 32], replicated, may hold values from -4 to 16, as said below
- coarse_lon: float32 [256, 256], replicated, may hold values from -4 to 16, as said below
Outputs:
- solution: float32 [4, 128, 1024], P(None, 'tile', 'mem')
- residual: float32 [4, 128, 1024], P(None, 'tile', 'mem')
Inputs may be any that keep to these rules, and one draw needn't show every extreme that they name: `coarse_lat`: symmetric. `coarse_lon`: symmetric.
All inputs are finite; a program needn't handle non-finite values.
Results may differ from a plain program's by a relative error of at most 0.0003.
Values may be sent and summed in bfloat16 or wider, within the bound.
A program may use at most 64 MiB of HBM per device.

v0:
```python
import jax
import jax.numpy as jnp
from jax import lax
from jax.sharding import PartitionSpec as P

ITERS = 2
exact_mode = lax.Precision.HIGHEST


def extended_2(array, sides, width):
    for axis, dim in sides:
        peers, length = (lax.axis_size(axis), array.shape[dim])
        up = [(i, (i + 1) % peers) for i in range(peers - 1)]
        down = [(j, i) for i, j in up]
        last = lax.slice_in_dim(array, length - width, length, axis=dim)
        first = lax.slice_in_dim(array, 0, width, axis=dim)
        before = lax.ppermute(last, axis, up)
        after = lax.ppermute(first, axis, down)
        array = jnp.concatenate([before, array, after], axis=dim)
    return array


def normalized(fine_taps):
    energy = fine_taps[:, :, 0] ** 2 + 2.0 * jnp.sum(fine_taps[:, :, 1:] ** 2, axis=2)
    return fine_taps / jnp.sqrt(energy)[:, :, None]


def lat_valid(values, kernel, height):
    result = kernel[None, :, 0, None, None] * values[:, :, 4 : 4 + height]
    for offset in range(1, 5):
        result = result + kernel[None, :, offset, None, None] * (
            values[:, :, 4 + offset : 4 + offset + height]
            + values[:, :, 4 - offset : 4 - offset + height]
        )
    return result


def lon_pass(values, kernel):
    result = kernel[None, :, 0, None, None] * values
    for offset in range(1, 5):
        result = result + kernel[None, :, offset, None, None] * (
            jnp.roll(values, offset, axis=3) + jnp.roll(values, -offset, axis=3)
        )
    return result


def shrink_table(extent):
    fine_index = jnp.arange(extent)[:, None] // 4
    coarse_index = jnp.arange(extent // 4)[None, :]
    return (fine_index == coarse_index).astype(jnp.float32) * 0.25


def expand_table(extent):
    coarse_index = jnp.arange(extent // 4)[:, None]
    fine_index = jnp.arange(extent)[None, :] // 4
    return (fine_index == coarse_index).astype(jnp.float32)


def block_mean(values):
    shape_now = values.shape
    lat_mean = (
        jnp.sum(
            values.reshape(shape_now[0], shape_now[1], shape_now[2] // 4, 4, shape_now[3]), axis=3
        )
        * 0.25
    )
    return jnp.einsum("abcd,de->abce", lat_mean, shrink_table(shape_now[3]), precision=exact_mode)


def prolong(coarse):
    shape_now = coarse.shape
    extent = shape_now[3] * 4
    widened = jnp.einsum("abce,ed->abcd", coarse, expand_table(extent), precision=exact_mode)
    spread_out = jnp.broadcast_to(
        widened[:, :, :, None, :], (shape_now[0], shape_now[1], shape_now[2], 4, extent)
    )
    return spread_out.reshape(shape_now[0], shape_now[1], shape_now[2] * 4, extent)


def local(perturbations, right_side, fine_taps, coarse_lat, coarse_lon):
    kernel = normalized(fine_taps)
    count_local, levels, height, extent = perturbations.shape
    groups = lax.axis_size("mem")
    members = count_local * groups
    share_width = extent // groups
    share_start = lax.axis_index("mem") * share_width
    tile_count = lax.axis_size("tile")
    residual_full = right_side
    residual = lax.dynamic_slice_in_dim(right_side, share_start, share_width, 2)
    solution = jnp.zeros_like(residual)
    squares = lax.psum(jnp.sum(residual * residual), ("mem", "tile"))
    for iteration in range(ITERS):
        weighted = perturbations.astype(jnp.float32) * residual_full[None]
        coarse = block_mean(weighted)
        apply_detail = weighted - prolong(coarse)
        coarse_items = coarse.reshape(
            tile_count, count_local * levels // tile_count, height // 4, extent // 4
        )
        across = jnp.einsum(
            "ab,skbc->skac",
            coarse_lat,
            lax.all_to_all(coarse_items, "tile", split_axis=0, concat_axis=2, tiled=True),
            precision=exact_mode,
        )
        smoothed = jnp.einsum("skac,cd->skad", across, coarse_lon, precision=exact_mode)
        detail = apply_detail
        for repeat in range(2):
            extended = extended_2(detail, (("tile", 2),), 4)
            detail = lat_valid(extended, kernel[0], height)
        apply_detail = detail
        apply_detail = lon_pass(lon_pass(apply_detail, kernel[1]), kernel[1])
        returned = lax.all_to_all(
            smoothed, "tile", split_axis=2, concat_axis=0, tiled=True
        ).reshape(count_local, levels, height // 4, extent // 4)
        blended = apply_detail - prolong(block_mean(apply_detail)) + prolong(returned)
        partial_value = jnp.sum(perturbations.astype(jnp.float32) * blended, axis=0)
        applied = residual + lax.psum_scatter(
            partial_value, "mem", scatter_dimension=2, tiled=True
        ) / (members - 1)
        step_size = squares / lax.psum(jnp.sum(residual * applied), ("mem", "tile"))
        solution = solution + step_size * residual
        residual = residual - step_size * applied
        if iteration + 1 < ITERS:
            squares = lax.psum(jnp.sum(residual * residual), ("mem", "tile"))
            residual_full = lax.all_gather(residual, "mem", axis=2, tiled=True)
    return (solution, residual)


def solution(mesh):
    placed = (P("mem", None, "tile", None), P(None, "tile", None), P(), P(), P())
    return jax.shard_map(
        local,
        mesh=mesh,
        in_specs=placed,
        out_specs=(P(None, "tile", "mem"), P(None, "tile", "mem")),
        check_vma=False,
    )
```

profile of v0, /device:TPU:0, one launch (start us, length us, event | category | flops | bytes accessed | tf_op | source)
XLA Modules:
  0.0 290.1 jit_solution(7245855886508990009)
XLA Ops:
  7.2 1.3 convert_multiply_fusion.3
  8.9 0.6 reduce_sum.101
  9.5 1.4 fusion.112
  10.9 1.3 fusion.129
  13.0 0.7 copy-done.2
  14.1 1.3 collective-permute-start
  15.4 5.6 %collective-permute-start.1 = (f32[2,4,4,1024]{3,2,1,0:T(4,128)S(1)}, f32[2,4,4,1024]{3,2,1,0:T(4,128)S(1)}, u32[]{:S(2)}, u32[]{:S(2)}) collective-permute-start(f32[2,4,4,1024]{3,2,1,0:T(4,128)S(1)} %get-tuple-element.91), channel_id=1, source_target_pairs={{0,1},{1,2},{2,3},{4,5},{5,6},{6,7},{8,9},{9,10},{10,11},{12,13},{... | collective-permute-start | bytes 393224 | tf_op jit(solution)/shard_map/ppermute | solution.py:17
  21.0 4.3 %all-to-all-start = ((f32[4,2,8,256]{3,2,1,0:T(8,128)}), f32[4,2,8,256]{3,2,1,0:T(8,128)S(1)}, u32[]{:S(2)}, u32[]{:S(2)}) async-start(f32[4,2,8,256]{3,2,1,0:T(8,128)} %bitcast.10), calls=%async_computation | async-start | bytes 131072 | tf_op jit(solution)/shard_map/all_to_all | solution.py:102
  26.1 4.9 %all-to-all-done = f32[4,2,8,256]{3,2,1,0:T(8,128)S(1)} async-done(((f32[4,2,8,256]{3,2,1,0:T(8,128)}), f32[4,2,8,256]{3,2,1,0:T(8,128)S(1)}, u32[]{:S(2)}, u32[]{:S(2)}) %all-to-all-start) | async-done | bytes 65568 | tf_op jit(solution)/shard_map/all_to_all | solution.py:102
  31.5 0.7 copy.19
  32.2 3.3 %all-to-all-start.1 = ((f32[1,2,32,256]{3,1,0,2:T(2,128)}), f32[1,2,32,256]{3,1,0,2:T(2,128)S(1)}, u32[]{:S(2)}, u32[]{:S(2)}) async-start(f32[1,2,32,256]{3,1,0,2:T(2,128)} %copy.19), calls=%async_computation.1 | async-start | bytes 131072 | tf_op jit(solution)/shard_map/all_to_all | solution.py:112
  35.6 0.6 copy-done.4
  36.2 2.5 fusion.52
  38.8 0.8 fusion.214
  39.5 1.3 collective-permute-start.2
  40.8 5.2 %collective-permute-start.3 = (f32[2,4,4,1024]{3,2,1,0:T(4,128)}, f32[2,4,4,1024]{3,2,1,0:T(4,128)}, u32[]{:S(2)}, u32[]{:S(2)}) collective-permute-start(f32[2,4,4,1024]{3,2,1,0:T(4,128)} %get-tuple-element.89), channel_id=1, source_target_pairs={{0,1},{1,2},{2,3},{4,5},{5,6},{6,7},{8,9},{9,10},{10,11},{12,13},{... | collective-permute-start | bytes 393224 | tf_op jit(solution)/shard_map/ppermute | solution.py:17
  46.0 0.5 fusion.125
  46.8 1.4 reshape.175
  48.2 2.5 fusion.36
  50.7 0.4 fusion.206
  51.1 0.4 fusion.208
  52.7 1.4 fusion.78
  54.1 0.4 fusion.198
  54.5 0.4 fusion.200
  56.1 1.4 fusion.86
  57.8 1.4 reduce_sum.102
  59.2 1.7 fusion.110
  61.0 0.5 fusion.127
  61.8 1.4 reshape.170
  63.2 2.7 fusion.64
  65.9 37.3 %reduce-scatter.3.cloned.1.call-done = f32[4,32,128]{2,1,0:T(8,128)} async-done(((f32[4,32,1024]{2,1,0:T(8,128)}), f32[4,32,128]{2,1,0:T(8,128)}) %reduce-scatter.3.cloned.1.call-update) | async-done | bytes 65552 | tf_op jit(solution)/shard_map/reduce_scatter | solution.py:117
  103.2 1.5 multiply_reduce_fusion.2
  104.7 39.5 %all-reduce.1 = (f32[]{:T(128)}, f32[]{:T(128)}) all-reduce(f32[]{:T(128)} %get-tuple-element.3, f32[]{:T(128)} %get-tuple-element.2), channel_id=1, replica_groups=mesh['mem'=8,'tile'=4] {'mem','tile'}, use_global_device_ids=true, to_apply=%region_1.0 | all-reduce | flops 2 | bytes 16 | tf_op jit(solution)/shard_map/psum | solution.py:91
  145.5 0.9 multiply_subtract_fusion.1
  146.4 12.1 %all_gather.3 = f32[4,32,1024]{2,1,0:T(8,128)S(1)} all-gather(f32[4,32,128]{2,1,0:T(8,128)S(1)} %multiply_subtract_fusion.1), channel_id=1, replica_groups=mesh['mem'=8,'tile'=4] {'mem'}, dimensions={2}, use_global_device_ids=true | all-gather | bytes 589824 | tf_op jit(solution)/shard_map/all_gather | solution.py:125
  158.9 0.6 reduce_sum.106
  159.6 1.4 fusion.108
  161.0 1.3 fusion.123
  163.3 3.8 %all-to-all-start.2 = ((f32[4,2,8,256]{3,2,1,0:T(8,128)}), f32[4,2,8,256]{3,2,1,0:T(8,128)S(1)}, u32[]{:S(2)}, u32[]{:S(2)}) async-start(f32[4,2,8,256]{3,2,1,0:T(8,128)} %bitcast.23), calls=%async_computation.3 | async-start | bytes 131072 | tf_op jit(solution)/shard_map/all_to_all | solution.py:102
  167.1 1.3 collective-permute-start.4
  168.4 4.6 %collective-permute-start.5 = (f32[2,4,4,1024]{3,2,1,0:T(4,128)S(1)}, f32[2,4,4,1024]{3,2,1,0:T(4,128)S(1)}, u32[]{:S(2)}, u32[]{:S(2)}) collective-permute-start(f32[2,4,4,1024]{3,2,1,0:T(4,128)S(1)} %get-tuple-element.55), channel_id=1, source_target_pairs={{0,1},{1,2},{2,3},{4,5},{5,6},{6,7},{8,9},{9,10},{10,11},{12,13},{... | collective-permute-start | bytes 393224 | tf_op jit(solution)/shard_map/ppermute | solution.py:17
  173.5 0.7 copy.22
  174.2 4.2 %all-to-all-start.3 = ((f32[1,2,32,256]{3,1,0,2:T(2,128)}), f32[1,2,32,256]{3,1,0,2:T(2,128)S(1)}, u32[]{:S(2)}, u32[]{:S(2)}) async-start(f32[1,2,32,256]{3,1,0,2:T(2,128)} %copy.22), calls=%async_computation.4 | async-start | bytes 131072 | tf_op jit(solution)/shard_map/all_to_all | solution.py:112
  178.4 1.4 fusion.20
  179.7 0.7 fusion.196
  180.4 1.3 collective-permute-start.6
  181.7 4.6 %collective-permute-start.7 = (f32[2,4,4,1024]{3,2,1,0:T(4,128)S(1)}, f32[2,4,4,1024]{3,2,1,0:T(4,128)S(1)}, u32[]{:S(2)}, u32[]{:S(2)}) collective-permute-start(f32[2,4,4,1024]{3,2,1,0:T(4,128)S(1)} %get-tuple-element.53), channel_id=1, source_target_pairs={{0,1},{1,2},{2,3},{4,5},{5,6},{6,7},{8,9},{9,10},{10,11},{12,13},{... | collective-permute-start | bytes 393224 | tf_op jit(solution)/shard_map/ppermute | solution.py:17
  186.3 0.5 fusion.119
  187.1 1.4 reshape.184
  188.8 1.3 fusion.4
  190.1 0.4 fusion.188
  190.9 0.4 fusion.192
  191.3 0.4 fusion.194
  192.1 1.4 fusion.94
  195.5 1.4 fusion.102
  197.3 0.6 reduce_sum.107
  197.9 0.8 fusion.106
  198.7 0.5 fusion.121
  199.5 1.4 reshape.179
  200.9 2.8 fusion.65
  203.7 35.6 %reduce-scatter.5.cloned.1.call-done = f32[4,32,128]{2,1,0:T(8,128)} async-done(((f32[4,32,1024]{2,1,0:T(8,128)}), f32[4,32,128]{2,1,0:T(8,128)}) %reduce-scatter.5.cloned.1.call-update) | async-done | bytes 65552 | tf_op jit(solution)/shard_map/reduce_scatter | solution.py:117
  239.3 1.5 multiply_reduce_fusion
  240.8 39.5 %all-reduce = (f32[]{:T(128)}, f32[]{:T(128)}) all-reduce(f32[]{:T(128)} %get-tuple-element.5, f32[]{:T(128)} %get-tuple-element.4), channel_id=1, replica_groups=mesh['mem'=8,'tile'=4] {'mem','tile'}, use_global_device_ids=true, to_apply=%region_10.11 | all-reduce | flops 2 | bytes 16 | tf_op jit(solution)/shard_map/psum | solution.py:124
  281.7 1.5 multiply_subtract_fusion
  (85 shorter events, 11.7 us)
Async XLA Ops:
  7.2 24.1 %copy-start = (f32[256,256]{1,0:T(8,128)S(1)}, f32[256,256]{1,0:T(8,128)}, u32[]{:S(2)}) copy-start(f32[256,256]{1,0:T(8,128)} %param.9) | copy-start | bytes 786436
  12.6 1.0 copy-start.2
  12.6 1.2 copy-start.3
  13.8 11.5 %copy-start.7 = (f32[2,4,5]{2,1,0:T(4,128)S(1)}, f32[2,4,5]{2,1,0:T(4,128)}, u32[]{:S(2)}) copy-start(f32[2,4,5]{2,1,0:T(4,128)} %param.7) | copy-start | bytes 484
  13.8 17.3 %copy-start.6 = (f32[32,32]{1,0:T(8,128)S(1)}, f32[32,32]{1,0:T(8,128)}, u32[]{:S(2)}) copy-start(f32[32,32]{1,0:T(8,128)} %param.8) | copy-start | bytes 12292
  14.1 21.5 %collective-permute-start = (f32[2,4,4,1024]{3,2,1,0:T(4,128)S(1)}, f32[2,4,4,1024]{3,2,1,0:T(4,128)S(1)}, u32[]{:S(2)}, u32[]{:S(2)}) collective-permute-start(f32[2,4,4,1024]{3,2,1,0:T(4,128)S(1)} %get-tuple-element.90), channel_id=1, source_target_pairs={{1,0},{2,1},{3,2},{5,4},{6,5},{7,6},{9,8},{10,9},{11,10},{13,12},{... | collective-permute-start | bytes 393224 | tf_op jit(solution)/shard_map/ppermute | solution.py:18
  15.4 20.2 %collective-permute-start.1 = (f32[2,4,4,1024]{3,2,1,0:T(4,128)S(1)}, f32[2,4,4,1024]{3,2,1,0:T(4,128)S(1)}, u32[]{:S(2)}, u32[]{:S(2)}) collective-permute-start(f32[2,4,4,1024]{3,2,1,0:T(4,128)S(1)} %get-tuple-element.91), channel_id=1, source_target_pairs={{0,1},{1,2},{2,3},{4,5},{5,6},{6,7},{8,9},{9,10},{10,11},{12,13},{... | collective-permute-start | bytes 393224 | tf_op jit(solution)/shard_map/ppermute | solution.py:17
  21.0 10.1 %all-to-all-start = ((f32[4,2,8,256]{3,2,1,0:T(8,128)}), f32[4,2,8,256]{3,2,1,0:T(8,128)S(1)}, u32[]{:S(2)}, u32[]{:S(2)}) async-start(f32[4,2,8,256]{3,2,1,0:T(8,128)} %bitcast.10), calls=%async_computation | async-start | bytes 131072 | tf_op jit(solution)/shard_map/all_to_all | solution.py:102
  32.2 13.9 %all-to-all-start.1 = ((f32[1,2,32,256]{3,1,0,2:T(2,128)}), f32[1,2,32,256]{3,1,0,2:T(2,128)S(1)}, u32[]{:S(2)}, u32[]{:S(2)}) async-start(f32[1,2,32,256]{3,1,0,2:T(2,128)} %copy.19), calls=%async_computation.1 | async-start | bytes 131072 | tf_op jit(solution)/shard_map/all_to_all | solution.py:112
  35.5 67.7 %reduce-scatter.3.cloned.1.call-start = ((), (), s32[]{:S(2)}) async-start(), calls=%async_computation.6 | async-start | bytes 589824 | tf_op jit(solution)/shard_map/reduce_scatter | solution.py:117
  35.5 0.7 copy-start.4
  35.6 0.7 copy-start.5
  39.5 8.7 %collective-permute-start.2 = (f32[2,4,4,1024]{3,2,1,0:T(4,128)}, f32[2,4,4,1024]{3,2,1,0:T(4,128)}, u32[]{:S(2)}, u32[]{:S(2)}) collective-permute-start(f32[2,4,4,1024]{3,2,1,0:T(4,128)} %get-tuple-element.88), channel_id=1, source_target_pairs={{1,0},{2,1},{3,2},{5,4},{6,5},{7,6},{9,8},{10,9},{11,10},{13,12},{... | collective-permute-start | bytes 393224 | tf_op jit(solution)/shard_map/ppermute | solution.py:18
  40.8 7.4 %collective-permute-start.3 = (f32[2,4,4,1024]{3,2,1,0:T(4,128)}, f32[2,4,4,1024]{3,2,1,0:T(4,128)}, u32[]{:S(2)}, u32[]{:S(2)}) collective-permute-start(f32[2,4,4,1024]{3,2,1,0:T(4,128)} %get-tuple-element.89), channel_id=1, source_target_pairs={{0,1},{1,2},{2,3},{4,5},{5,6},{6,7},{8,9},{9,10},{10,11},{12,13},{... | collective-permute-start | bytes 393224 | tf_op jit(solution)/shard_map/ppermute | solution.py:17
  163.3 9.8 %all-to-all-start.2 = ((f32[4,2,8,256]{3,2,1,0:T(8,128)}), f32[4,2,8,256]{3,2,1,0:T(8,128)S(1)}, u32[]{:S(2)}, u32[]{:S(2)}) async-start(f32[4,2,8,256]{3,2,1,0:T(8,128)} %bitcast.23), calls=%async_computation.3 | async-start | bytes 131072 | tf_op jit(solution)/shard_map/all_to_all | solution.py:102
  167.1 11.2 %collective-permute-start.4 = (f32[2,4,4,1024]{3,2,1,0:T(4,128)S(1)}, f32[2,4,4,1024]{3,2,1,0:T(4,128)S(1)}, u32[]{:S(2)}, u32[]{:S(2)}) collective-permute-start(f32[2,4,4,1024]{3,2,1,0:T(4,128)S(1)} %get-tuple-element.54), channel_id=1, source_target_pairs={{1,0},{2,1},{3,2},{5,4},{6,5},{7,6},{9,8},{10,9},{11,10},{13,12},{... | collective-permute-start | bytes 393224 | tf_op jit(solution)/shard_map/ppermute | solution.py:18
  168.4 9.9 %collective-permute-start.5 = (f32[2,4,4,1024]{3,2,1,0:T(4,128)S(1)}, f32[2,4,4,1024]{3,2,1,0:T(4,128)S(1)}, u32[]{:S(2)}, u32[]{:S(2)}) collective-permute-start(f32[2,4,4,1024]{3,2,1,0:T(4,128)S(1)} %get-tuple-element.55), channel_id=1, source_target_pairs={{0,1},{1,2},{2,3},{4,5},{5,6},{6,7},{8,9},{9,10},{10,11},{12,13},{... | collective-permute-start | bytes 393224 | tf_op jit(solution)/shard_map/ppermute | solution.py:17
  174.2 12.1 %all-to-all-start.3 = ((f32[1,2,32,256]{3,1,0,2:T(2,128)}), f32[1,2,32,256]{3,1,0,2:T(2,128)S(1)}, u32[]{:S(2)}, u32[]{:S(2)}) async-start(f32[1,2,32,256]{3,1,0,2:T(2,128)} %copy.22), calls=%async_computation.4 | async-start | bytes 131072 | tf_op jit(solution)/shard_map/all_to_all | solution.py:112
  178.4 61.0 %reduce-scatter.5.cloned.1.call-start = ((), (), s32[]{:S(2)}) async-start(), calls=%async_computation.7 | async-start | bytes 589824 | tf_op jit(solution)/shard_map/reduce_scatter | solution.py:117
  180.4 8.0 %collective-permute-start.6 = (f32[2,4,4,1024]{3,2,1,0:T(4,128)}, f32[2,4,4,1024]{3,2,1,0:T(4,128)S(1)}, u32[]{:S(2)}, u32[]{:S(2)}) collective-permute-start(f32[2,4,4,1024]{3,2,1,0:T(4,128)} %get-tuple-element.52), channel_id=1, source_target_pairs={{1,0},{2,1},{3,2},{5,4},{6,5},{7,6},{9,8},{10,9},{11,10},{13,12},{... | collective-permute-start | bytes 393224 | tf_op jit(solution)/shard_map/ppermute | solution.py:18
  181.7 7.1 %collective-permute-start.7 = (f32[2,4,4,1024]{3,2,1,0:T(4,128)S(1)}, f32[2,4,4,1024]{3,2,1,0:T(4,128)S(1)}, u32[]{:S(2)}, u32[]{:S(2)}) collective-permute-start(f32[2,4,4,1024]{3,2,1,0:T(4,128)S(1)} %get-tuple-element.53), channel_id=1, source_target_pairs={{0,1},{1,2},{2,3},{4,5},{5,6},{6,7},{8,9},{9,10},{10,11},{12,13},{... | collective-permute-start | bytes 393224 | tf_op jit(solution)/shard_map/ppermute | solution.py:17
  200.9 82.3 %copy-start.1 = (f32[256,256]{1,0:T(8,128)S(1)}, f32[256,256]{1,0:T(8,128)}, u32[]{:S(2)}) copy-start(f32[256,256]{1,0:T(8,128)} %param.9) | copy-start | bytes 786436
Sparse Core Ops, SparseCore 0:
  66.1 37.0 reduce-scatter.2
  203.9 35.4 reduce-scatter.4
where the time goes:
time: 291 us; the launch traced here: 290 us
  blocking collectives  91.2 us (31%)
  waiting for transfers between devices  78.2 us (27%)
  starting transfers between devices  40.7 us (14%)
  other arithmetic  29.8 us (10%)
  local copies, waits for them, and re-layouts  21.9 us (8%)
  between operations  17.4 us (6%)
  matrix products  11 us (4%)
    psum x2, blocking collectives, local(): squares = lax.psum(jnp.sum(residual * residual), ('mem', 'tile'))  79.1 us
    reduce_scatter x2, waiting for transfers between devices, local(): lax.psum_scatter(partial_value, 'mem', scatter_dimension=2, tiled=True)  72.9 us
    ppermute x4, starting transfers between devices, extended_2(): before = lax.ppermute(last, axis, up)  19.9 us
    all_gather x1, blocking collectives, local(): residual_full = lax.all_gather(residual, 'mem', axis=2, tiled=True)  12.1 us
    all_to_all x2, starting transfers between devices, local(): lax.all_to_all(coarse_items, 'tile', split_axis=0, concat_axis=2, tiled=T...  8.15 us
    add x4, other arithmetic, lat_valid(): result + kernel[None, :, offset, None, None] * (values[:, :, 4 + offset:4...  7.76 us
    slice x32, local copies, waits for them, and re-layouts, lon_pass(): jnp.roll(values, -offset, axis=3)  7.69 us
    all_to_all x2, starting transfers between devices, local(): lax.all_to_all(smoothed, 'tile', split_axis=2, concat_axis=0, tiled=True)  7.47 us
  transfers between devices with their start and end apart: 14, of which 4 were waited for; matrix products, arithmetic and copies ran while one was open for 4% of the time, Pallas kernels for 0%

commit v1 on v0

--- a/solution.py
+++ b/solution.py
@@ -5,6 +5,15 @@
 
 ITERS = 2
 exact_mode = lax.Precision.HIGHEST
+
+
+def keys_note(m, dim_at, array_axis):
+    arr_out = lax.axis_size("tile")
+    o_now = jnp.split(m, arr_out, axis=dim_at)
+    taken_in = jnp.stack(o_now)
+    x_now = lax.all_to_all(taken_in, "tile", 0, 0)
+    h_now = jnp.concatenate(x_now, axis=array_axis)
+    return h_now
 
 
 def extended_2(array, sides, width):
@@ -109,9 +118,9 @@
             detail = lat_valid(extended, kernel[0], height)
         apply_detail = detail
         apply_detail = lon_pass(lon_pass(apply_detail, kernel[1]), kernel[1])
-        returned = lax.all_to_all(
-            smoothed, "tile", split_axis=2, concat_axis=0, tiled=True
-        ).reshape(count_local, levels, height // 4, extent // 4)
+        returned = keys_note(smoothed, dim_at=2, array_axis=0).reshape(
+            count_local, levels, height // 4, extent // 4
+        )
         blended = apply_detail - prolong(block_mean(apply_detail)) + prolong(returned)
         partial_value = jnp.sum(perturbations.astype(jnp.float32) * blended, axis=0)
         applied = residual + lax.psum_scatter(

time: 291 us -> 291 us (level)
  no operation moved by 1% of the time
where the time goes in v1:
time: 291 us; the launch traced here: 290 us
  blocking collectives  91.1 us (31%)
  waiting for transfers between devices  78.3 us (27%)
  starting transfers between devices  40.7 us (14%)
  other arithmetic  31.1 us (11%)
  local copies, waits for them, and re-layouts  20.4 us (7%)
  between operations  17.4 us (6%)
  matrix products  11 us (4%)
    psum x2, blocking collectives, local(): squares = lax.psum(jnp.sum(residual * residual), ('mem', 'tile'))  79 us
    reduce_scatter x2, waiting for transfers between devices, local(): lax.psum_scatter(partial_value, 'mem', scatter_dimension=2, tiled=True)  72.9 us
    ppermute x4, starting transfers between devices, extended_2(): before = lax.ppermute(last, axis, up)  19.9 us
    all_gather x1, blocking collectives, local(): residual_full = lax.all_gather(residual, 'mem', axis=2, tiled=True)  12.1 us
    all_to_all x2, starting transfers between devices, local(): lax.all_to_all(coarse_items, 'tile', split_axis=0, concat_axis=2, tiled=T...  8.15 us
    add x4, other arithmetic, lat_valid(): result + kernel[None, :, offset, None, None] * (values[:, :, 4 + offset:4...  7.84 us
    slice x32, local copies, waits for them, and re-layouts, lon_pass(): jnp.roll(values, -offset, axis=3)  7.69 us
    all_to_all x2, starting transfers between devices, keys_note(): x_now = lax.all_to_all(taken_in, 'tile', 0, 0)  7.47 us
  transfers between devices with their start and end apart: 14, of which 4 were waited for; matrix products, arithmetic and copies ran while one was open for 4% of the time, Pallas kernels for 0%

profile of v1, /device:TPU:0, one launch (start us, length us, event | category | flops | bytes accessed | tf_op | source)
XLA Modules:
  0.0 290.0 jit_solution(13487958482676459193)
XLA Ops:
  7.2 1.3 convert_multiply_fusion.3
  8.9 0.6 reduce_sum.101
  9.5 1.4 fusion.112
  10.9 1.3 fusion.129
  13.0 0.7 copy-done.2
  14.1 1.3 collective-permute-start
  15.4 5.6 %collective-permute-start.1 = (f32[2,4,4,1024]{3,2,1,0:T(4,128)S(1)}, f32[2,4,4,1024]{3,2,1,0:T(4,128)S(1)}, u32[]{:S(2)}, u32[]{:S(2)}) collective-permute-start(f32[2,4,4,1024]{3,2,1,0:T(4,128)S(1)} %get-tuple-element.91), channel_id=1, source_target_pairs={{0,1},{1,2},{2,3},{4,5},{5,6},{6,7},{8,9},{9,10},{10,11},{12,13},{... | collective-permute-start | bytes 393224 | tf_op jit(solution)/shard_map/ppermute | solution.py:26
  21.0 4.3 %all-to-all-start = ((f32[4,2,8,256]{3,2,1,0:T(8,128)}), f32[4,2,8,256]{3,2,1,0:T(8,128)S(1)}, u32[]{:S(2)}, u32[]{:S(2)}) async-start(f32[4,2,8,256]{3,2,1,0:T(8,128)} %bitcast.10), calls=%async_computation | async-start | bytes 131072 | tf_op jit(solution)/shard_map/all_to_all | solution.py:111
  26.1 4.9 %all-to-all-done = f32[4,2,8,256]{3,2,1,0:T(8,128)S(1)} async-done(((f32[4,2,8,256]{3,2,1,0:T(8,128)}), f32[4,2,8,256]{3,2,1,0:T(8,128)S(1)}, u32[]{:S(2)}, u32[]{:S(2)}) %all-to-all-start) | async-done | bytes 65568 | tf_op jit(solution)/shard_map/all_to_all | solution.py:111
  31.5 0.6 pad_maximum_fusion.8
  32.2 3.3 %all-to-all-start.1 = ((f32[4,1,2,8,256]{4,3,2,1,0:T(8,128)}), f32[4,1,2,8,256]{4,3,2,1,0:T(8,128)S(1)}, u32[]{:S(2)}, u32[]{:S(2)}) async-start(f32[4,1,2,8,256]{4,3,2,1,0:T(8,128)} %pad_maximum_fusion.8), calls=%async_computation.1 | async-start | bytes 131072 | tf_op jit(solution)/shard_map/all_to_all | solution.py:14
  35.5 0.6 copy-done.4
  36.2 2.5 fusion.52
  38.7 0.8 fusion.214
  39.5 1.3 collective-permute-start.2
  40.8 5.2 %collective-permute-start.3 = (f32[2,4,4,1024]{3,2,1,0:T(4,128)}, f32[2,4,4,1024]{3,2,1,0:T(4,128)}, u32[]{:S(2)}, u32[]{:S(2)}) collective-permute-start(f32[2,4,4,1024]{3,2,1,0:T(4,128)} %get-tuple-element.89), channel_id=1, source_target_pairs={{0,1},{1,2},{2,3},{4,5},{5,6},{6,7},{8,9},{9,10},{10,11},{12,13},{... | collective-permute-start | bytes 393224 | tf_op jit(solution)/shard_map/ppermute | solution.py:26
  46.0 0.5 fusion.125
  46.8 1.3 reshape.166
  48.2 2.6 fusion.36
  51.6 0.4 fusion.210
  52.0 0.4 fusion.212
  52.8 1.4 fusion.78
  55.0 0.4 fusion.202
  55.4 0.4 fusion.204
  56.2 1.4 fusion.86
  57.9 1.4 reduce_sum.102
  59.3 1.7 fusion.110
  61.0 0.5 fusion.127
  61.8 1.4 reshape.162
  63.2 2.7 fusion.64
  66.0 37.3 %reduce-scatter.3.cloned.1.call-done = f32[4,32,128]{2,1,0:T(8,128)} async-done(((f32[4,32,1024]{2,1,0:T(8,128)}), f32[4,32,128]{2,1,0:T(8,128)}) %reduce-scatter.3.cloned.1.call-update) | async-done | bytes 65552 | tf_op jit(solution)/shard_map/reduce_scatter | solution.py:126
  103.3 1.5 multiply_reduce_fusion.2
  104.7 39.5 %all-reduce.1 = (f32[]{:T(128)}, f32[]{:T(128)}) all-reduce(f32[]{:T(128)} %get-tuple-element.3, f32[]{:T(128)} %get-tuple-element.2), channel_id=1, replica_groups=mesh['mem'=8,'tile'=4] {'mem','tile'}, use_global_device_ids=true, to_apply=%region_1.0 | all-reduce | flops 2 | bytes 16 | tf_op jit(solution)/shard_map/psum | solution.py:100
  145.6 0.9 multiply_subtract_fusion.1
  146.4 12.1 %all_gather.3 = f32[4,32,1024]{2,1,0:T(8,128)S(1)} all-gather(f32[4,32,128]{2,1,0:T(8,128)S(1)} %multiply_subtract_fusion.1), channel_id=1, replica_groups=mesh['mem'=8,'tile'=4] {'mem'}, dimensions={2}, use_global_device_ids=true | all-gather | bytes 589824 | tf_op jit(solution)/shard_map/all_gather | solution.py:134
  159.0 0.6 reduce_sum.106
  159.6 1.4 fusion.108
  161.0 1.3 fusion.123
  163.3 3.8 %all-to-all-start.2 = ((f32[4,2,8,256]{3,2,1,0:T(8,128)}), f32[4,2,8,256]{3,2,1,0:T(8,128)S(1)}, u32[]{:S(2)}, u32[]{:S(2)}) async-start(f32[4,2,8,256]{3,2,1,0:T(8,128)} %bitcast.25), calls=%async_computation.3 | async-start | bytes 131072 | tf_op jit(solution)/shard_map/all_to_all | solution.py:111
  167.2 1.3 collective-permute-start.4
  168.5 4.6 %collective-permute-start.5 = (f32[2,4,4,1024]{3,2,1,0:T(4,128)S(1)}, f32[2,4,4,1024]{3,2,1,0:T(4,128)S(1)}, u32[]{:S(2)}, u32[]{:S(2)}) collective-permute-start(f32[2,4,4,1024]{3,2,1,0:T(4,128)S(1)} %get-tuple-element.55), channel_id=1, source_target_pairs={{0,1},{1,2},{2,3},{4,5},{5,6},{6,7},{8,9},{9,10},{10,11},{12,13},{... | collective-permute-start | bytes 393224 | tf_op jit(solution)/shard_map/ppermute | solution.py:26
  173.5 0.6 pad_maximum_fusion.9
  174.2 4.2 %all-to-all-start.3 = ((f32[4,1,2,8,256]{4,3,2,1,0:T(8,128)}), f32[4,1,2,8,256]{4,3,2,1,0:T(8,128)S(1)}, u32[]{:S(2)}, u32[]{:S(2)}) async-start(f32[4,1,2,8,256]{4,3,2,1,0:T(8,128)} %pad_maximum_fusion.9), calls=%async_computation.4 | async-start | bytes 131072 | tf_op jit(solution)/shard_map/all_to_all | solution.py:14
  178.4 1.4 fusion.20
  179.7 0.7 fusion.196
  180.4 1.3 collective-permute-start.6
  181.7 4.6 %collective-permute-start.7 = (f32[2,4,4,1024]{3,2,1,0:T(4,128)S(1)}, f32[2,4,4,1024]{3,2,1,0:T(4,128)S(1)}, u32[]{:S(2)}, u32[]{:S(2)}) collective-permute-start(f32[2,4,4,1024]{3,2,1,0:T(4,128)S(1)} %get-tuple-element.53), channel_id=1, source_target_pairs={{0,1},{1,2},{2,3},{4,5},{5,6},{6,7},{8,9},{9,10},{10,11},{12,13},{... | collective-permute-start | bytes 393224 | tf_op jit(solution)/shard_map/ppermute | solution.py:26
  186.3 0.5 fusion.119
  187.1 1.3 reshape.174
  188.8 1.3 fusion.4
  190.1 0.4 fusion.188
  190.5 0.4 fusion.190
  192.1 1.4 fusion.94
  193.6 0.4 fusion.180
  195.5 1.4 fusion.102
  197.3 0.6 reduce_sum.107
  197.9 0.8 fusion.106
  198.7 0.5 fusion.121
  199.5 1.4 reshape.170
  200.9 2.8 fusion.65
  203.7 35.6 %reduce-scatter.5.cloned.1.call-done = f32[4,32,128]{2,1,0:T(8,128)} async-done(((f32[4,32,1024]{2,1,0:T(8,128)}), f32[4,32,128]{2,1,0:T(8,128)}) %reduce-scatter.5.cloned.1.call-update) | async-done | bytes 65552 | tf_op jit(solution)/shard_map/reduce_scatter | solution.py:126
  239.3 1.5 multiply_reduce_fusion
  240.8 39.5 %all-reduce = (f32[]{:T(128)}, f32[]{:T(128)}) all-reduce(f32[]{:T(128)} %get-tuple-element.5, f32[]{:T(128)} %get-tuple-element.4), channel_id=1, replica_groups=mesh['mem'=8,'tile'=4] {'mem','tile'}, use_global_device_ids=true, to_apply=%region_10.11 | all-reduce | flops 2 | bytes 16 | tf_op jit(solution)/shard_map/psum | solution.py:133
  281.6 1.5 multiply_subtract_fusion
  (85 shorter events, 11.7 us)
Async XLA Ops:
  7.2 24.1 %copy-start = (f32[256,256]{1,0:T(8,128)S(1)}, f32[256,256]{1,0:T(8,128)}, u32[]{:S(2)}) copy-start(f32[256,256]{1,0:T(8,128)} %param.9) | copy-start | bytes 786436
  12.6 1.0 copy-start.2
  12.6 1.2 copy-start.3
  13.8 11.5 %copy-start.7 = (f32[2,4,5]{2,1,0:T(4,128)S(1)}, f32[2,4,5]{2,1,0:T(4,128)}, u32[]{:S(2)}) copy-start(f32[2,4,5]{2,1,0:T(4,128)} %param.7) | copy-start | bytes 484
  13.8 17.3 %copy-start.6 = (f32[32,32]{1,0:T(8,128)S(1)}, f32[32,32]{1,0:T(8,128)}, u32[]{:S(2)}) copy-start(f32[32,32]{1,0:T(8,128)} %param.8) | copy-start | bytes 12292
  14.1 21.4 %collective-permute-start = (f32[2,4,4,1024]{3,2,1,0:T(4,128)S(1)}, f32[2,4,4,1024]{3,2,1,0:T(4,128)S(1)}, u32[]{:S(2)}, u32[]{:S(2)}) collective-permute-start(f32[2,4,4,1024]{3,2,1,0:T(4,128)S(1)} %get-tuple-element.90), channel_id=1, source_target_pairs={{1,0},{2,1},{3,2},{5,4},{6,5},{7,6},{9,8},{10,9},{11,10},{13,12},{... | collective-permute-start | bytes 393224 | tf_op jit(solution)/shard_map/ppermute | solution.py:27
  15.4 20.1 %collective-permute-start.1 = (f32[2,4,4,1024]{3,2,1,0:T(4,128)S(1)}, f32[2,4,4,1024]{3,2,1,0:T(4,128)S(1)}, u32[]{:S(2)}, u32[]{:S(2)}) collective-permute-start(f32[2,4,4,1024]{3,2,1,0:T(4,128)S(1)} %get-tuple-element.91), channel_id=1, source_target_pairs={{0,1},{1,2},{2,3},{4,5},{5,6},{6,7},{8,9},{9,10},{10,11},{12,13},{... | collective-permute-start | bytes 393224 | tf_op jit(solution)/shard_map/ppermute | solution.py:26
  21.0 10.1 %all-to-all-start = ((f32[4,2,8,256]{3,2,1,0:T(8,128)}), f32[4,2,8,256]{3,2,1,0:T(8,128)S(1)}, u32[]{:S(2)}, u32[]{:S(2)}) async-start(f32[4,2,8,256]{3,2,1,0:T(8,128)} %bitcast.10), calls=%async_computation | async-start | bytes 131072 | tf_op jit(solution)/shard_map/all_to_all | solution.py:111
  32.2 13.9 %all-to-all-start.1 = ((f32[4,1,2,8,256]{4,3,2,1,0:T(8,128)}), f32[4,1,2,8,256]{4,3,2,1,0:T(8,128)S(1)}, u32[]{:S(2)}, u32[]{:S(2)}) async-start(f32[4,1,2,8,256]{4,3,2,1,0:T(8,128)} %pad_maximum_fusion.8), calls=%async_computation.1 | async-start | bytes 131072 | tf_op jit(solution)/shard_map/all_to_all | solution.py:14
  35.4 67.8 %reduce-scatter.3.cloned.1.call-start = ((), (), s32[]{:S(2)}) async-start(), calls=%async_computation.6 | async-start | bytes 589824 | tf_op jit(solution)/shard_map/reduce_scatter | solution.py:126
  35.5 0.6 copy-start.4
  35.5 0.7 copy-start.5
  39.5 8.6 %collective-permute-start.2 = (f32[2,4,4,1024]{3,2,1,0:T(4,128)}, f32[2,4,4,1024]{3,2,1,0:T(4,128)}, u32[]{:S(2)}, u32[]{:S(2)}) collective-permute-start(f32[2,4,4,1024]{3,2,1,0:T(4,128)} %get-tuple-element.88), channel_id=1, source_target_pairs={{1,0},{2,1},{3,2},{5,4},{6,5},{7,6},{9,8},{10,9},{11,10},{13,12},{... | collective-permute-start | bytes 393224 | tf_op jit(solution)/shard_map/ppermute | solution.py:27
  40.8 7.4 %collective-permute-start.3 = (f32[2,4,4,1024]{3,2,1,0:T(4,128)}, f32[2,4,4,1024]{3,2,1,0:T(4,128)}, u32[]{:S(2)}, u32[]{:S(2)}) collective-permute-start(f32[2,4,4,1024]{3,2,1,0:T(4,128)} %get-tuple-element.89), channel_id=1, source_target_pairs={{0,1},{1,2},{2,3},{4,5},{5,6},{6,7},{8,9},{9,10},{10,11},{12,13},{... | collective-permute-start | bytes 393224 | tf_op jit(solution)/shard_map/ppermute | solution.py:26
  163.3 9.8 %all-to-all-start.2 = ((f32[4,2,8,256]{3,2,1,0:T(8,128)}), f32[4,2,8,256]{3,2,1,0:T(8,128)S(1)}, u32[]{:S(2)}, u32[]{:S(2)}) async-start(f32[4,2,8,256]{3,2,1,0:T(8,128)} %bitcast.25), calls=%async_computation.3 | async-start | bytes 131072 | tf_op jit(solution)/shard_map/all_to_all | solution.py:111
  167.2 11.2 %collective-permute-start.4 = (f32[2,4,4,1024]{3,2,1,0:T(4,128)S(1)}, f32[2,4,4,1024]{3,2,1,0:T(4,128)S(1)}, u32[]{:S(2)}, u32[]{:S(2)}) collective-permute-start(f32[2,4,4,1024]{3,2,1,0:T(4,128)S(1)} %get-tuple-element.54), channel_id=1, source_target_pairs={{1,0},{2,1},{3,2},{5,4},{6,5},{7,6},{9,8},{10,9},{11,10},{13,12},{... | collective-permute-start | bytes 393224 | tf_op jit(solution)/shard_map/ppermute | solution.py:27
  168.5 9.9 %collective-permute-start.5 = (f32[2,4,4,1024]{3,2,1,0:T(4,128)S(1)}, f32[2,4,4,1024]{3,2,1,0:T(4,128)S(1)}, u32[]{:S(2)}, u32[]{:S(2)}) collective-permute-start(f32[2,4,4,1024]{3,2,1,0:T(4,128)S(1)} %get-tuple-element.55), channel_id=1, source_target_pairs={{0,1},{1,2},{2,3},{4,5},{5,6},{6,7},{8,9},{9,10},{10,11},{12,13},{... | collective-permute-start | bytes 393224 | tf_op jit(solution)/shard_map/ppermute | solution.py:26
  174.2 12.1 %all-to-all-start.3 = ((f32[4,1,2,8,256]{4,3,2,1,0:T(8,128)}), f32[4,1,2,8,256]{4,3,2,1,0:T(8,128)S(1)}, u32[]{:S(2)}, u32[]{:S(2)}) async-start(f32[4,1,2,8,256]{4,3,2,1,0:T(8,128)} %pad_maximum_fusion.9), calls=%async_computation.4 | async-start | bytes 131072 | tf_op jit(solution)/shard_map/all_to_all | solution.py:14
  178.4 61.0 %reduce-scatter.5.cloned.1.call-start = ((), (), s32[]{:S(2)}) async-start(), calls=%async_computation.7 | async-start | bytes 589824 | tf_op jit(solution)/shard_map/reduce_scatter | solution.py:126
  180.4 8.0 %collective-permute-start.6 = (f32[2,4,4,1024]{3,2,1,0:T(4,128)}, f32[2,4,4,1024]{3,2,1,0:T(4,128)S(1)}, u32[]{:S(2)}, u32[]{:S(2)}) collective-permute-start(f32[2,4,4,1024]{3,2,1,0:T(4,128)} %get-tuple-element.52), channel_id=1, source_target_pairs={{1,0},{2,1},{3,2},{5,4},{6,5},{7,6},{9,8},{10,9},{11,10},{13,12},{... | collective-permute-start | bytes 393224 | tf_op jit(solution)/shard_map/ppermute | solution.py:27
  181.7 7.1 %collective-permute-start.7 = (f32[2,4,4,1024]{3,2,1,0:T(4,128)S(1)}, f32[2,4,4,1024]{3,2,1,0:T(4,128)S(1)}, u32[]{:S(2)}, u32[]{:S(2)}) collective-permute-start(f32[2,4,4,1024]{3,2,1,0:T(4,128)S(1)} %get-tuple-element.53), channel_id=1, source_target_pairs={{0,1},{1,2},{2,3},{4,5},{5,6},{6,7},{8,9},{9,10},{10,11},{12,13},{... | collective-permute-start | bytes 393224 | tf_op jit(solution)/shard_map/ppermute | solution.py:26
  200.9 82.3 %copy-start.1 = (f32[256,256]{1,0:T(8,128)S(1)}, f32[256,256]{1,0:T(8,128)}, u32[]{:S(2)}) copy-start(f32[256,256]{1,0:T(8,128)} %param.9) | copy-start | bytes 786436
Sparse Core Ops, SparseCore 0:
  66.1 37.1 reduce-scatter.2
  203.8 35.4 reduce-scatter.4
